TPU v7x, 32 devices: a whole 2x2x4 slice. The times are simulated.
32 devices in a mesh: dp: 16 (over z, x, core), rep: 2 (over y).
Axes of the slice: x: 2, y: 2, z: 4, core: 2. Of those that a mesh axis runs over, the one named last changes fastest.
Arguments:
- tokens: bfloat16 [48, 261, 768], P('dp'), may hold values from -6 to 6
- text_len: int32 [48], P('dp'), may hold values from 1 to 64, as said below
- routes: int32 [48, 261], P('dp'), may hold values from 0 to 2, as said below
- attn_gain: float32 [768], replicated, may hold values from 0.5 to 1.5
- attn_shift: float32 [768], replicated, may hold values from -1 to 1
- w_qkv: bfloat16 [3, 768, 768], P(None, 'dp', 'rep'), may hold values from -0.21875 to 0.21875
- b_qv: float32 [2, 768], P(None, 'rep'), may hold values from -1.5 to 1.5
- w_out: bfloat16 [768, 768], P('dp', 'rep'), may hold values from -1.25 to 1.25
- b_out: float32 [768], replicated, may hold values from -0.5 to 0.5
- ffn_gain: float32 [768], replicated, may hold values from 0.5 to 1.5
- ffn_shift: float32 [768], replicated, may hold values from -1 to 1
- w_up: bfloat16 [3, 768, 3072], P(None, 'dp', 'rep'), may hold values from -0.21875 to 0.21875
- b_up: float32 [3, 3072], P(None, 'rep'), may hold values from -1.5 to 1.5
- w_down: bfloat16 [3, 768, 3072], P(None, 'dp', 'rep'), may hold values from -0.15625 to 0.15625
- b_down: float32 [3, 768], replicated, may hold values from -0.5 to 0.5
- cotangent: bfloat16 [48, 261, 768], P('dp'), may hold values from -6 to 6
Outputs:
- output: bfloat16 [48, 261, 768], P('dp')
- grad_tokens: float32 [48, 261, 768], P('dp')
- grad_w_qkv: float32 [3, 768, 768], P(None, 'dp', 'rep')
- grad_w_out: float32 [768, 768], P('dp', 'rep')
- grad_w_up: float32 [3, 768, 3072], P(None, 'dp', 'rep')
- grad_w_down: float32 [3, 768, 3072], P(None, 'dp', 'rep')
- grad_b_qv: float32 [2, 768], P(None, 'rep')
- grad_b_out: float32 [768], replicated
- grad_b_up: float32 [3, 3072], P(None, 'rep')
- grad_b_down: float32 [3, 768], replicated
- grad_norms: float32 [4, 768], replicated
Inputs may be any that keep to these rules, and one draw needn't show every extreme that they name: `text_len`: text rows in use of each item; some item uses all 64 in every draw. `routes`: routing by modality: each item either sends its first 197 rows to expert 0 and its other rows to expert 1, or sends all its rows to expert 2; both kinds of item occur in every draw.
All inputs are finite; a program needn't handle non-finite values.
Results may differ from a plain program's by a relative error of at most 0.014.
Values may be sent and summed in bfloat16 or wider, within the bound.
No kernel may reach another device: no remote copies, remote signals or barrier semaphores. Data moves between devices by JAX's collectives and lax.ppermute only.
A program may use at most 192 MiB of HBM per device.

v0:
```python
import math
import jax
import jax.numpy as jnp
from jax import lax
from jax.sharding import PartitionSpec as P

HDIM = 64
IMG = 197
EPSILON = 1e-05
TILE = 128
ROOT_HALF = 0.7071067811865476
INV_ROOT_TAU = 0.3989422804014327
HIGHEST = lax.Precision.HIGHEST


def norm_rows(vector, gain_vec, shift_vec):
    row_mean = jnp.mean(vector, axis=-1, keepdims=True)
    centred = vector - row_mean
    row_var = jnp.mean(centred * centred, axis=-1, keepdims=True)
    spread = lax.rsqrt(row_var + EPSILON)
    normal_rows = centred * spread
    return (normal_rows * gain_vec + shift_vec, normal_rows, spread)


def norm_back(grad_rows, normal_rows, spread, gain_vec):
    scaled = grad_rows * gain_vec
    return spread * (
        scaled
        - jnp.mean(scaled, axis=-1, keepdims=True)
        - normal_rows * jnp.mean(scaled * normal_rows, axis=-1, keepdims=True)
    )


def gelu_slope(pre_act):
    return (
        0.5 * (1.0 + lax.erf(pre_act * ROOT_HALF))
        + pre_act * jnp.exp(-0.5 * pre_act * pre_act) * INV_ROOT_TAU
    )


def packing(route_flat, expert_count, row_count):
    tile_count = -(-row_count // TILE) + expert_count
    route_hits = (route_flat[:, None] == jnp.arange(expert_count, dtype=jnp.int32)[None, :]).astype(
        jnp.int32
    )
    counts = jnp.sum(route_hits, axis=0)
    padded = (counts + TILE - 1) // TILE * TILE
    group_end = jnp.cumsum(padded)
    group_start = group_end - padded
    before = jnp.cumsum(route_hits, axis=0) - route_hits
    target = jnp.sum(route_hits * (before + group_start[None, :]), axis=1)
    tile_start = jnp.arange(tile_count, dtype=jnp.int32) * TILE
    tile_owner = jnp.minimum(
        jnp.sum((tile_start[:, None] >= group_end[None, :]).astype(jnp.int32), axis=1),
        expert_count - 1,
    )
    return (target, tile_owner, tile_count)


def per_device(
    tokens,
    text_len,
    routes,
    attn_gain,
    attn_shift,
    w_qkv,
    b_qv,
    w_out,
    b_out,
    ffn_gain,
    ffn_shift,
    w_up,
    b_up,
    w_down,
    b_down,
    cotangent,
):
    item_count, seq_len, model_width = tokens.shape
    row_count = item_count * seq_len
    local_width = w_qkv.shape[2]
    local_heads = local_width // HDIM
    expert_count = w_up.shape[0]
    score_scale = 1.0 / math.sqrt(HDIM)
    contract_last = (((1,), (1,)), ((), ()))
    contract_first = (((0,), (0,)), ((), ()))
    inputs = tokens.reshape(row_count, model_width).astype(jnp.float32)
    first_normed, first_hat, first_spread = norm_rows(inputs, attn_gain, attn_shift)
    first_low = first_normed.astype(jnp.bfloat16)
    qkv_full, out_full = (
        lax.all_gather(w_qkv, "dp", axis=1, tiled=True),
        lax.all_gather(w_out, "dp", axis=0, tiled=True),
    )
    projected = jnp.einsum("rd,tde->tre", first_low, qkv_full, preferred_element_type=jnp.float32)
    bias_rows = jnp.stack([b_qv[0], jnp.zeros_like(b_qv[0]), b_qv[1]])
    proj_low = (projected + bias_rows[:, None, :]).astype(jnp.bfloat16)
    head_split = proj_low.reshape(3, item_count, seq_len, local_heads, HDIM)
    queries, key_rows, values = (head_split[0], head_split[1], head_split[2])
    key_ok = jnp.arange(seq_len, dtype=jnp.int32)[None, :] < (IMG + text_len)[:, None]

    def scores_of(query_part, key_part):
        raw_scores = (
            jnp.einsum("ishd,ijhd->ihsj", query_part, key_part, preferred_element_type=jnp.float32)
            * score_scale
        )
        return jnp.where(key_ok[:, None, None, :], raw_scores, -1e30)

    raw_scores = scores_of(queries, key_rows)
    row_max = jnp.max(raw_scores, axis=-1, keepdims=True)
    raised = jnp.exp(raw_scores - row_max)
    row_total = jnp.sum(raised, axis=-1, keepdims=True)
    attn_probs = raised / row_total
    log_total = row_max + jnp.log(row_total)
    probs_low = attn_probs.astype(jnp.bfloat16)
    context = jnp.einsum("ihsj,ijhd->ishd", probs_low, values, preferred_element_type=jnp.float32)
    context_low = context.reshape(row_count, local_width).astype(jnp.bfloat16)
    attn_part = lax.dot_general(
        context_low, out_full, contract_last, preferred_element_type=jnp.float32
    )
    attn_share = lax.psum_scatter(
        attn_part.astype(jnp.bfloat16), "rep", scatter_dimension=1, tiled=True
    ).astype(jnp.float32)
    attn_sum = lax.all_gather(attn_share.astype(jnp.bfloat16), "rep", axis=1, tiled=True).astype(
        attn_share.dtype
    )
    residual = inputs + (attn_sum + b_out)
    second_normed, second_hat, second_spread = norm_rows(residual, ffn_gain, ffn_shift)
    second_low = second_normed.astype(jnp.bfloat16)
    route_flat = routes.reshape(row_count)
    target, tile_owner, tile_count = packing(route_flat, expert_count, row_count)
    packed_input = (
        jnp.zeros((tile_count * TILE, model_width), jnp.bfloat16)
        .at[target]
        .set(second_low)
        .reshape(tile_count, TILE, model_width)
    )
    up_full, down_full = (
        lax.all_gather(w_up, "dp", axis=1, tiled=True),
        lax.all_gather(w_down, "dp", axis=1, tiled=True),
    )
    owner_hot = (tile_owner[:, None] == jnp.arange(expert_count, dtype=jnp.int32)[None, :]).astype(
        jnp.float32
    )
    up_projection_tiles = up_full[tile_owner]
    down_projection_tiles = down_full[tile_owner]
    pre_acts = (
        jnp.einsum(
            "pim,pmj->pij", packed_input, up_projection_tiles, preferred_element_type=jnp.float32
        )
        + jnp.dot(owner_hot, b_up, precision=HIGHEST)[:, None, :]
    )
    activated_rows = jax.nn.gelu(pre_acts, approximate=False).astype(jnp.bfloat16)
    partial_sums = jnp.einsum(
        "wmy,wny->wmn", activated_rows, down_projection_tiles, preferred_element_type=jnp.float32
    )
    ffn_rows = partial_sums.reshape(tile_count * TILE, model_width)[target]
    ffn_share = lax.psum_scatter(
        ffn_rows.astype(jnp.bfloat16), "rep", scatter_dimension=1, tiled=True
    ).astype(jnp.float32)
    ffn_sum = lax.all_gather(ffn_share.astype(jnp.bfloat16), "rep", axis=1, tiled=True).astype(
        ffn_share.dtype
    )
    route_pick = (route_flat[:, None] == jnp.arange(expert_count, dtype=jnp.int32)[None, :]).astype(
        jnp.float32
    )
    output = residual + (ffn_sum + jnp.dot(route_pick, b_down, precision=HIGHEST))
    output_low = output.astype(jnp.bfloat16).reshape(item_count, seq_len, model_width)
    grad_low = cotangent.reshape(row_count, model_width)
    grad_out = grad_low.astype(jnp.float32)
    grad_b_down = jnp.dot(route_pick.T, grad_out, precision=HIGHEST)
    up_back, down_back, qkv_back, out_back = (
        lax.all_gather(w_up, "dp", axis=1, tiled=True),
        lax.all_gather(w_down, "dp", axis=1, tiled=True),
        lax.all_gather(w_qkv, "dp", axis=1, tiled=True),
        lax.all_gather(w_out, "dp", axis=0, tiled=True),
    )
    up_gradient_tiles = up_back[tile_owner]
    down_gradient_tiles = down_back[tile_owner]
    packed_gradient = (
        jnp.zeros((tile_count * TILE, model_width), jnp.bfloat16)
        .at[target]
        .set(grad_low)
        .reshape(tile_count, TILE, model_width)
    )
    grad_active = jnp.einsum(
        "pim,pmj->pij", packed_gradient, down_gradient_tiles, preferred_element_type=jnp.float32
    )
    gradient_before_activation = (grad_active * gelu_slope(pre_acts)).astype(jnp.bfloat16)
    grad_tiles = jnp.einsum(
        "wmy,wny->wmn",
        gradient_before_activation,
        up_gradient_tiles,
        preferred_element_type=jnp.float32,
    )
    down_terms = jnp.einsum(
        "jxa,jxm->jam", packed_gradient, activated_rows, preferred_element_type=jnp.float32
    )
    grad_down_local = jnp.einsum("te,tdf->edf", owner_hot, down_terms, precision=HIGHEST)
    up_projection_terms = jnp.einsum(
        "jxa,jxm->jam", packed_input, gradient_before_activation, preferred_element_type=jnp.float32
    )
    grad_up_local = jnp.einsum("te,tdf->edf", owner_hot, up_projection_terms, precision=HIGHEST)
    grad_b_up = jnp.dot(
        owner_hot.T,
        jnp.sum(gradient_before_activation.astype(jnp.float32), axis=1),
        precision=HIGHEST,
    )
    back_rows = grad_tiles.reshape(tile_count * TILE, model_width)[target]
    second_share = lax.psum_scatter(
        back_rows.astype(jnp.bfloat16), "rep", scatter_dimension=1, tiled=True
    ).astype(jnp.float32)
    grad_second = lax.all_gather(
        second_share.astype(jnp.bfloat16), "rep", axis=1, tiled=True
    ).astype(second_share.dtype)
    grad_ffn_gain = jnp.sum(grad_second * second_hat, axis=0)
    grad_ffn_shift = jnp.sum(grad_second, axis=0)
    grad_residual = grad_out + norm_back(grad_second, second_hat, second_spread, ffn_gain)
    grad_w_up, grad_w_down = (
        lax.psum_scatter(grad_up_local, "dp", scatter_dimension=1, tiled=True),
        lax.psum_scatter(grad_down_local, "dp", scatter_dimension=1, tiled=True),
    )
    grad_branch = grad_residual.astype(jnp.bfloat16)
    grad_b_out = jnp.sum(grad_branch.astype(jnp.float32), axis=0)
    grad_context = jnp.dot(grad_branch, out_back, preferred_element_type=jnp.float32)
    grad_ctx_low = grad_context.astype(jnp.bfloat16).reshape(item_count, seq_len, local_heads, HDIM)
    grad_out_local = lax.dot_general(
        grad_branch, context_low, contract_first, preferred_element_type=jnp.float32
    )
    again_scores = scores_of(queries, key_rows)
    again_probs = jnp.exp(again_scores - log_total)
    again_low = again_probs.astype(jnp.bfloat16)
    grad_probs = jnp.einsum(
        "ishd,ijhd->ihsj", grad_ctx_low, values, preferred_element_type=jnp.float32
    )
    grad_values = jnp.einsum(
        "ihsj,ishd->ijhd", again_low, grad_ctx_low, preferred_element_type=jnp.float32
    )
    inner_sum = jnp.sum(again_probs * grad_probs, axis=-1, keepdims=True)
    grad_scores = (again_probs * (grad_probs - inner_sum)).astype(jnp.bfloat16)
    grad_queries = (
        jnp.einsum("ihsj,ijhd->ishd", grad_scores, key_rows, preferred_element_type=jnp.float32)
        * score_scale
    )
    grad_keys = (
        jnp.einsum("ihsj,ishd->ijhd", grad_scores, queries, preferred_element_type=jnp.float32)
        * score_scale
    )
    grad_proj = (
        jnp.stack([grad_queries, grad_keys, grad_values])
        .reshape(3, row_count, local_width)
        .astype(jnp.bfloat16)
    )
    grad_b_qv = jnp.stack(
        [
            jnp.sum(grad_proj[0].astype(jnp.float32), axis=0),
            jnp.sum(grad_proj[2].astype(jnp.float32), axis=0),
        ]
    )
    grad_qkv_local = jnp.einsum(
        "rd,tre->tde", first_low, grad_proj, preferred_element_type=jnp.float32
    )
    back_first = jnp.einsum("tre,tde->rd", grad_proj, qkv_back, preferred_element_type=jnp.float32)
    first_share = lax.psum_scatter(
        back_first.astype(jnp.bfloat16), "rep", scatter_dimension=1, tiled=True
    ).astype(jnp.float32)
    grad_first = lax.all_gather(first_share.astype(jnp.bfloat16), "rep", axis=1, tiled=True).astype(
        first_share.dtype
    )
    grad_attn_gain = jnp.sum(grad_first * first_hat, axis=0)
    grad_attn_shift = jnp.sum(grad_first, axis=0)
    grad_inputs = grad_residual + norm_back(grad_first, first_hat, first_spread, attn_gain)
    grad_w_qkv, grad_w_out = (
        lax.psum_scatter(grad_qkv_local, "dp", scatter_dimension=1, tiled=True),
        lax.psum_scatter(grad_out_local, "dp", scatter_dimension=0, tiled=True),
    )
    norm_local = jnp.stack([grad_attn_gain, grad_attn_shift, grad_ffn_gain, grad_ffn_shift])
    total_qv, total_out, total_up, total_down, total_norms = lax.psum(
        (grad_b_qv, grad_b_out, grad_b_up, grad_b_down, norm_local), "dp"
    )
    return (
        output_low,
        grad_inputs.reshape(item_count, seq_len, model_width),
        grad_w_qkv,
        grad_w_out,
        grad_w_up,
        grad_w_down,
        total_qv,
        total_out,
        total_up,
        total_down,
        total_norms,
    )


def solution(mesh):
    return jax.shard_map(
        per_device,
        mesh=mesh,
        in_specs=(
            P("dp", None, None),
            P("dp"),
            P("dp", None),
            P(),
            P(),
            P(None, "dp", "rep"),
            P(None, "rep"),
            P("dp", "rep"),
            P(),
            P(),
            P(),
            P(None, "dp", "rep"),
            P(None, "rep"),
            P(None, "dp", "rep"),
            P(),
            P("dp", None, None),
        ),
        out_specs=(
            P("dp", None, None),
            P("dp", None, None),
            P(None, "dp", "rep"),
            P("dp", "rep"),
            P(None, "dp", "rep"),
            P(None, "dp", "rep"),
            P(None, "rep"),
            P(),
            P(None, "rep"),
            P(),
            P(),
        ),
        check_vma=False,
    )
```

profile of v0, /device:TPU:0, one launch (start us, length us, event | category | flops | bytes accessed | tf_op | source)
XLA Modules:
  0.0 1421.6 jit_solution(17374396237260171322)
XLA Ops:
  14.2 27.1 %all_gather.29 = bf16[768,384]{1,0:T(8,128)(2,1)} all-gather(bf16[48,384]{1,0:T(8,128)(2,1)S(1)} %copy-done.33), channel_id=1, replica_groups=mesh['dp'=16,'rep'=2] {'dp'}, dimensions={0}, use_global_device_ids=true | all-gather | bytes 626688 | tf_op jit(solution)/shard_map/all_gather | solution.py:91
  41.3 13.2 all-gather.8.cloned.1.call-done
  79.3 22.8 %reduce-scatter.16.cloned.1.call-done = bf16[384,783]{1,0:T(8,128)(2,1)} async-done(((bf16[768,783]{1,0:T(8,128)(2,1)}), bf16[384,783]{1,0:T(8,128)(2,1)}) %reduce-scatter.16.cloned.1.call-update) | async-done | bytes 601360
  116.8 10.7 all-gather.10.cloned.1.call-done
  130.4 7.9 scatter_custom_fusion
  138.2 57.4 %all-gather.12.cloned.1.call-done = bf16[3,768,1536]{2,1,0:T(8,128)(2,1)} async-done(((bf16[3,48,1536]{2,1,0:T(8,128)(2,1)}), bf16[3,768,1536]{2,1,0:T(8,128)(2,1)}) %all-gather.12.cloned.1.call-update) | async-done | bytes 7077904 | tf_op jit(solution)/shard_map/all_gather | solution.py:137
  202.1 8.3 gather_fusion.2
  210.5 7.8 gather_fusion.3
  218.3 10.3 constant_dynamic-update-slice_fusion.1
  228.6 34.1 %all-gather.14.cloned.1.call-done = bf16[3,768,1536]{2,1,0:T(8,128)(2,1)} async-done(((bf16[3,48,1536]{2,1,0:T(8,128)(2,1)}), bf16[3,768,1536]{2,1,0:T(8,128)(2,1)}) %all-gather.14.cloned.1.call-update) | async-done | bytes 7077904 | tf_op jit(solution)/shard_map/all_gather | solution.py:138
  277.0 10.1 constant_dynamic-update-slice_fusion.3
  294.9 10.6 constant_dynamic-update-slice_fusion
  312.3 14.1 fusion.22
  326.3 15.7 %convert_reduce_fusion = (f32[10,1536]{1,0:T(8,128)}, bf16[10,128,1536]{2,1,0:T(8,128)(2,1)}) fusion(f32[10,128,1536]{2,1,0:T(8,128)} %get-tuple-element.99, f32[10,1536]{1,0:T(8,128)S(1)} %fusion.73, bf16[10,128,768]{2,1,0:T(8,128)(2,1)S(1)} %bitcast.105, bf16[10,768,1536]{2,1,0:T(8,128)(2,1)} %constant_dynamic-update-slice_fusion.2), kind=kOutput, calls=%fused_computation.28 | convolution fusion | flops 3045442560 | bytes 37478400 | tf_op jit(solution)/shard_map/pim,pmj->pij/dot_general | solution.py:184
  342.0 13.8 fusion.100
  364.9 20.1 %fusion.6 = bf16[10,128,1536]{2,1,0:T(8,128)(2,1)} fusion(f32[10,128,1536]{2,1,0:T(8,128)} %get-tuple-element.99, f32[10,1536]{1,0:T(8,128)S(1)} %fusion.73, u16[128,1536]{1,0:T(8,128)(2,1)} %get-tuple-element.67, u16[128,1536]{1,0:T(8,128)(2,1)} %get-tuple-element.66), kind=kLoop, calls=%fused_computation.16 | loop fusion | flops 139591680 | bytes 12644352 | tf_op jit(solution)/shard_map/convert_element_type | solution.py:151
  385.0 13.7 fusion.99
  410.0 20.8 %fusion.101 = f32[10,768,1536]{2,1,0:T(8,128)} fusion(bf16[10,128,768]{2,1,0:T(8,128)(2,1)} %bitcast.103, bf16[10,128,1536]{2,1,0:T(8,128)(2,1)} %get-tuple-element.103), kind=kOutput, calls=%fused_computation.193 | convolution fusion | flops 3019898880 | bytes 53084160 | tf_op jit(solution)/shard_map/jxa,jxm->jam/dot_general | solution.py:198
  476.3 67.0 %fusion.2 = f32[3,768,1536]{2,0,1:T(4,128)} fusion(f32[10,768,1536]{2,1,0:T(8,128)} %fusion.101, s32[10]{0:T(128)S(1)} %copy-done.43), kind=kOutput, calls=%fused_computation.10 | convolution fusion | flops 424673312 | bytes 61341736 | tf_op jit(solution)/shard_map/te,tdf->edf/dot_general | solution.py:201
  545.6 21.0 %fusion.102 = f32[10,768,1536]{2,1,0:T(8,128)} fusion(bf16[10,128,768]{2,1,0:T(8,128)(2,1)S(1)} %bitcast.106, bf16[10,128,1536]{2,1,0:T(8,128)(2,1)} %fusion.6), kind=kOutput, calls=%fused_computation.194 | convolution fusion | flops 3019898880 | bytes 53084160 | tf_op jit(solution)/shard_map/jxa,jxm->jam/dot_general | solution.py:194
  568.9 67.0 %fusion = f32[3,768,1536]{2,0,1:T(4,128)} fusion(f32[10,768,1536]{2,1,0:T(8,128)} %fusion.102, s32[10]{0:T(128)S(1)} %copy-done.43), kind=kOutput, calls=%fused_computation.8 | convolution fusion | flops 424673312 | bytes 61341736 | tf_op jit(solution)/shard_map/te,tdf->edf/dot_general | solution.py:197
  671.5 65.2 %all-reduce.4 = (f32[2,384]{1,0:T(2,128)}, f32[768]{0:T(1024)}, f32[3,1536]{1,0:T(4,128)}, f32[3,768]{1,0:T(4,128)}, f32[4,768]{1,0:T(4,128)}) all-reduce(f32[2,384]{1,0:T(2,128)S(1)} %pad_maximum_fusion.5, f32[768]{0:T(1024)S(1)} %get-tuple-element.84, f32[3,1536]{1,0:T(4,128)S(1)} %fusion.71, ...), channel_id=1, replica_groups=mesh['dp'=16,'rep'=2] {'dp'}, use_global_device_ids=true, to_apply=%region_29.30 | all-reduce | flops 11520 | bytes 92160 | tf_op jit(solution)/shard_map/psum | solution.py:276
  736.8 615.4 %all-reduce.8.cloned.1.call-done = (f32[3,768,384]{2,0,1:T(4,128)}, f32[3,768,1536]{2,0,1:T(4,128)}, f32[3,768,1536]{2,0,1:T(4,128)}) async-done(((f32[3,768,384]{2,0,1:T(4,128)}, f32[3,768,1536]{2,0,1:T(4,128)}, f32[3,768,1536]{2,0,1:T(4,128)}), (f32[3,768,384]{2,0,1:T(4,128)}, f32[3,768,1536]{2,0,1:T(4,128)}, f32[3,768,1536]{2,0,1:T(4,128)})) %all-reduce.8.cloned.1.call-update) | async-done | bytes 31850512
  1359.2 55.4 %reduce-scatter.14.cloned.1.call-done = f32[48,384]{1,0:T(8,128)} async-done(((f32[768,384]{1,0:T(8,128)}), f32[48,384]{1,0:T(8,128)}) %reduce-scatter.14.cloned.1.call-update) | async-done | bytes 73744 | tf_op jit(solution)/shard_map/reduce_scatter | solution.py:273
  (260 shorter events, 196.2 us)
Async XLA Ops:
  7.2 109.3 %copy-start = (f32[3,1536]{1,0:T(4,128)S(1)}, f32[3,1536]{1,0:T(4,128)}, u32[]{:S(2)}) copy-start(f32[3,1536]{1,0:T(4,128)} %param.28) | copy-start | bytes 55300
  7.2 47.3 %copy-start.48 = (f32[768]{0:T(1024)S(1)}, f32[768]{0:T(1024)}, u32[]{:S(2)}) copy-start(f32[768]{0:T(1024)} %param.20) | copy-start | bytes 9220
  7.2 47.2 %all-gather.8.cloned.1.call-start = ((), (), s32[]{:S(2)}) async-start(), calls=%async_computation.5 | async-start | bytes 1880064 | tf_op jit(solution)/shard_map/all_gather | solution.py:90
  8.0 94.1 %reduce-scatter.16.cloned.1.call-start = ((), (), s32[]{:S(2)}) async-start(), calls=%async_computation.13 | async-start | bytes 2064384
  9.6 48.4 %copy-start.6 = (f32[783,768]{1,0:T(8,128)}, f32[783,768]{1,0:T(8,128)S(1)}, u32[]{:S(2)}) copy-start(f32[783,768]{1,0:T(8,128)S(1)} %reshape.320) | copy-start | bytes 7216132
  79.2 48.2 %all-gather.10.cloned.1.call-start = ((), (), s32[]{:S(2)}) async-start(), calls=%async_computation.6 | async-start | bytes 1806336 | tf_op jit(solution)/shard_map/all_gather | solution.py:122
  104.3 91.4 %all-gather.12.cloned.1.call-start = ((), (), s32[]{:S(2)}) async-start(), calls=%async_computation.7 | async-start | bytes 7520256 | tf_op jit(solution)/shard_map/all_gather | solution.py:137
  104.8 157.8 %all-gather.14.cloned.1.call-start = ((), (), s32[]{:S(2)}) async-start(), calls=%async_computation.8 | async-start | bytes 7520256 | tf_op jit(solution)/shard_map/all_gather | solution.py:138
  105.4 302.3 %reduce-scatter.20.cloned.1.call-start = ((), (), s32[]{:S(2)}) async-start(), calls=%async_computation.15 | async-start | bytes 2064384
  129.9 304.6 %copy-start.3 = (f32[783,768]{1,0:T(8,128)}, f32[783,768]{1,0:T(8,128)S(1)}, u32[]{:S(2)}) copy-start(f32[783,768]{1,0:T(8,128)S(1)} %get-tuple-element.87) | copy-start | bytes 7216132
  364.8 67.0 %all-gather.18.cloned.1.call-start = ((), (), s32[]{:S(2)}) async-start(), calls=%async_computation.10 | async-start | bytes 1806336 | tf_op jit(solution)/shard_map/all_gather | solution.py:211
  410.0 133.4 %reduce-scatter.18.cloned.1.call-start = ((), (), s32[]{:S(2)}) async-start(), calls=%async_computation.14 | async-start | bytes 2064384
  430.8 135.8 %reduce-scatter.22.cloned.1.call-start = ((), (), s32[]{:S(2)}) async-start(), calls=%async_computation.16 | async-start | bytes 2064384
  476.2 69.3 %copy-start.20 = (bf16[1280,768]{1,0:T(8,128)(2,1)S(1)}, bf16[1280,768]{1,0:T(8,128)(2,1)}, u32[]{:S(2)}) copy-start(bf16[1280,768]{1,0:T(8,128)(2,1)} %scatter_custom_fusion.1) | copy-start | bytes 5898244
  476.2 175.0 %all-gather.16.cloned.1.call-start = ((), (), s32[]{:S(2)}) async-start(), calls=%async_computation.9 | async-start | bytes 1806336 | tf_op jit(solution)/shard_map/all_gather | solution.py:159
  545.5 117.8 %all-gather.20.cloned.1.call-start = ((), (), s32[]{:S(2)}) async-start(), calls=%async_computation.11 | async-start | bytes 1806336 | tf_op jit(solution)/shard_map/all_gather | solution.py:265
  568.8 67.1 %copy-start.7 = (f32[783,768]{1,0:T(8,128)S(1)}, f32[783,768]{1,0:T(8,128)}, u32[]{:S(2)}) copy-start(f32[783,768]{1,0:T(8,128)} %copy-done.6) | copy-start | bytes 7216132
  568.8 67.1 %copy-start.36 = (f32[783]{0:T(1024)S(1)}, f32[783]{0:T(1024)}, u32[]{:S(2)}) copy-start(f32[783]{0:T(1024)} %copy-done.35) | copy-start | bytes 9400
  568.8 67.1 %copy-start.38 = (f32[783]{0:T(1024)S(1)}, f32[783]{0:T(1024)}, u32[]{:S(2)}) copy-start(f32[783]{0:T(1024)} %copy-done.37) | copy-start | bytes 9400
  568.8 67.1 %copy-start.40 = (f32[768]{0:T(1024)S(1)}, f32[768]{0:T(1024)}, u32[]{:S(2)}) copy-start(f32[768]{0:T(1024)} %param.19) | copy-start | bytes 9220
  568.8 67.1 %copy-start.49 = (f32[768]{0:T(1024)S(1)}, f32[768]{0:T(1024)}, u32[]{:S(2)}) copy-start(f32[768]{0:T(1024)} %param.20) | copy-start | bytes 9220
  568.9 783.3 %all-reduce.8.cloned.1.call-start = ((), (), s32[]{:S(2)}) async-start(), calls=%async_computation.17 | async-start | bytes 84934656
  647.7 767.0 %reduce-scatter.14.cloned.1.call-start = ((), (), s32[]{:S(2)}) async-start(), calls=%async_computation.12 | async-start | bytes 1253376 | tf_op jit(solution)/shard_map/reduce_scatter | solution.py:273
  1353.9 60.8 %copy-start.1 = (f32[3,1536]{1,0:T(4,128)S(1)}, f32[3,1536]{1,0:T(4,128)}, u32[]{:S(2)}) copy-start(f32[3,1536]{1,0:T(4,128)} %param.28) | copy-start | bytes 55300
  (43 other events, 413.5 us)
Sparse Core Ops, SparseCore 0:
  10.4 44.0 all-gather.7
  79.4 22.6 reduce-scatter.15
  104.4 23.0 all-gather.9
  129.6 66.0 all-gather.11
  197.8 64.8 all-gather.13
  365.0 22.7 reduce-scatter.19
  410.1 21.7 all-gather.17
  434.1 23.9 reduce-scatter.17
  476.4 24.2 reduce-scatter.21
  545.6 23.2 all-gather.15
  570.5 23.0 all-gather.19
  647.8 704.3 all-reduce.7
  1356.3 58.2 reduce-scatter.13
where the time goes:
time: 1430 us; the launch traced here: 1420 us
  waiting for transfers between devices  812 us (57%)
  matrix products  278 us (19%)
  local copies, waits for them, and re-layouts  171 us (12%)
  blocking collectives  92.3 us (6%)
  other arithmetic  52.2 us (4%)
  between operations  16 us (1%)
    unnamed x18, waiting for transfers between devices  640 us
    unnamed x128, local copies, waits for them, and re-layouts  67.2 us
    dot_general x1, matrix products, per_device(): jnp.einsum('te,tdf->edf', owner_hot, up_projection_terms, precision=HIGHEST)  67 us
    dot_general x1, matrix products, per_device(): jnp.einsum('te,tdf->edf', owner_hot, down_terms, precision=HIGHEST)  67 us
    psum x1, blocking collectives, per_device(): lax.psum((grad_b_qv, grad_b_out, grad_b_up, grad_b_down, norm_local), 'dp')  65.2 us
    all_gather x1, waiting for transfers between devices, per_device(): lax.all_gather(w_up, 'dp', axis=1, tiled=True)  57.4 us
    reduce_scatter x1, waiting for transfers between devices, per_device(): lax.psum_scatter(grad_out_local, 'dp', scatter_dimension=0, tiled=True)  55.4 us
    all_gather x1, waiting for transfers between devices, per_device(): lax.all_gather(w_down, 'dp', axis=1, tiled=True)  34.1 us
  transfers between devices with their start and end apart: 13, of which 8 were waited for; matrix products, arithmetic and copies ran while one was open for 26% of the time, Pallas kernels for 0%

commit v1 on v0

--- a/solution.py
+++ b/solution.py
@@ -11,6 +11,25 @@
 ROOT_HALF = 0.7071067811865476
 INV_ROOT_TAU = 0.3989422804014327
 HIGHEST = lax.Precision.HIGHEST
+
+
+def search_levels_all_by_axis(arr_in, comm_axis):
+    piece_now, arr_next, block_last = (
+        lax.axis_size(comm_axis),
+        lax.axis_index(comm_axis),
+        arr_in.shape[1],
+    )
+    gallery = [(dd, (dd + 1) % piece_now) for dd in range(piece_now)]
+    tile_out = jnp.zeros(
+        (*arr_in.shape[:1], piece_now * block_last, *arr_in.shape[2:]), arr_in.dtype
+    )
+    block_now = arr_in
+    for dev_j in range(piece_now):
+        a_next = (arr_next - dev_j) % piece_now
+        tile_out = lax.dynamic_update_slice_in_dim(tile_out, block_now, a_next * block_last, axis=1)
+        if dev_j < piece_now - 1:
+            block_now = lax.ppermute(block_now, axis_name=comm_axis, perm=gallery)
+    return tile_out
 
 
 def norm_rows(vector, gain_vec, shift_vec):
@@ -135,7 +154,7 @@
     )
     up_full, down_full = (
         lax.all_gather(w_up, "dp", axis=1, tiled=True),
-        lax.all_gather(w_down, "dp", axis=1, tiled=True),
+        search_levels_all_by_axis(w_down, "dp"),
     )
     owner_hot = (tile_owner[:, None] == jnp.arange(expert_count, dtype=jnp.int32)[None, :]).astype(
         jnp.float32

time: 1430 us -> 1530 us (1.070)
  waiting for transfers between devices: 812 us -> 902 us
    ppermute x0 -> x15, waiting for transfers between devices: none -> 196 us  [search_levels_all_by_axis(): block_now = lax.ppermute(block_now, axis_name=comm_axis, perm=gallery)]
    all_gather x1, waiting for transfers between devices: 57.4 us -> 0.02 us  [per_device(): lax.all_gather(w_up, 'dp', axis=1, tiled=True)]
    all_gather x1, waiting for transfers between devices: 34.1 us -> 0.01 us  [per_device(): lax.all_gather(w_down, 'dp', axis=1, tiled=True)]
    gather x0 -> x3, local copies, waits for them, and re-layouts: none -> 22.3 us  [per_device(): down_gradient_tiles = down_back[tile_owner]]
    unnamed x128 -> x116, local copies, waits for them, and re-layouts: 67.2 us -> 49.9 us
  transfers between devices with their start and end apart: 13 -> 28, of which waited for: 8 -> 19; matrix products, arithmetic and copies ran while one was open for 26% -> 26% of each run, Pallas kernels for 0% -> 0%
where the time goes in v1:
time: 1530 us
  waiting for transfers between devices  902 us (59%)
  matrix products  281 us (18%)
  local copies, waits for them, and re-layouts  181 us (12%)
  blocking collectives  91.6 us (6%)
  other arithmetic  55.2 us (4%)
  between operations  16.3 us (1%)
    unnamed x18, waiting for transfers between devices  639 us
    ppermute x15, waiting for transfers between devices, search_levels_all_by_axis(): block_now = lax.ppermute(block_now, axis_name=comm_axis, perm=gallery)  196 us
    dot_general x1, matrix products, per_device(): jnp.einsum('te,tdf->edf', owner_hot, down_terms, precision=HIGHEST)  66.9 us
    dot_general x1, matrix products, per_device(): jnp.einsum('te,tdf->edf', owner_hot, up_projection_terms, precision=HIGHEST)  66.8 us
    psum x1, blocking collectives, per_device(): lax.psum((grad_b_qv, grad_b_out, grad_b_up, grad_b_down, norm_local), 'dp')  64.8 us
    reduce_scatter x1, waiting for transfers between devices, per_device(): lax.psum_scatter(grad_out_local, 'dp', scatter_dimension=0, tiled=True)  55.4 us
    unnamed x116, local copies, waits for them, and re-layouts  49.9 us
  transfers between devices with their start and end apart: 28, of which 19 were waited for; matrix products, arithmetic and copies ran while one was open for 26% of the time, Pallas kernels for 0%

profile of v1, /device:TPU:0, one launch (start us, length us, event | category | flops | bytes accessed | tf_op | source)
XLA Modules:
  0.0 1527.8 jit_solution(11013524337678914541)
XLA Ops:
  15.6 26.8 %all_gather.28 = bf16[768,384]{1,0:T(8,128)(2,1)} all-gather(bf16[48,384]{1,0:T(8,128)(2,1)} %param.23), channel_id=1, replica_groups=mesh['dp'=16,'rep'=2] {'dp'}, dimensions={0}, use_global_device_ids=true | all-gather | bytes 626688 | tf_op jit(solution)/shard_map/all_gather | solution.py:110
  42.4 12.3 all-gather.8.cloned.1.call-done
  80.4 22.8 %reduce-scatter.16.cloned.1.call-done = bf16[384,783]{1,0:T(8,128)(2,1)} async-done(((bf16[768,783]{1,0:T(8,128)(2,1)}), bf16[384,783]{1,0:T(8,128)(2,1)}) %reduce-scatter.16.cloned.1.call-update) | async-done | bytes 601360
  106.7 10.4 collective-permute-done
  139.5 16.6 %collective-permute-done.3 = bf16[3,48,1536]{2,1,0:T(8,128)(2,1)S(1)} collective-permute-done((bf16[3,48,1536]{2,1,0:T(8,128)(2,1)S(1)}, bf16[3,48,1536]{2,1,0:T(8,128)(2,1)S(1)}, u32[]{:S(2)}, u32[]{:S(2)}) %collective-permute-start.3) | collective-permute-done | bytes 442400 | tf_op jit(solution)/shard_map/ppermute | solution.py:31
  167.5 18.7 %collective-permute-done.5 = bf16[3,48,1536]{2,1,0:T(8,128)(2,1)S(1)} collective-permute-done((bf16[3,48,1536]{2,1,0:T(8,128)(2,1)}, bf16[3,48,1536]{2,1,0:T(8,128)(2,1)S(1)}, u32[]{:S(2)}, u32[]{:S(2)}) %collective-permute-start.5) | collective-permute-done | bytes 442400 | tf_op jit(solution)/shard_map/ppermute | solution.py:31
  186.8 15.7 %collective-permute-done.6 = bf16[3,48,1536]{2,1,0:T(8,128)(2,1)S(1)} collective-permute-done((bf16[3,48,1536]{2,1,0:T(8,128)(2,1)S(1)}, bf16[3,48,1536]{2,1,0:T(8,128)(2,1)S(1)}, u32[]{:S(2)}, u32[]{:S(2)}) %collective-permute-start.6) | collective-permute-done | bytes 442400 | tf_op jit(solution)/shard_map/ppermute | solution.py:31
  202.8 13.3 collective-permute-done.7
  227.7 18.9 %collective-permute-done.9 = bf16[3,48,1536]{2,1,0:T(8,128)(2,1)S(1)} collective-permute-done((bf16[3,48,1536]{2,1,0:T(8,128)(2,1)S(1)}, bf16[3,48,1536]{2,1,0:T(8,128)(2,1)S(1)}, u32[]{:S(2)}, u32[]{:S(2)}) %collective-permute-start.9) | collective-permute-done | bytes 442400 | tf_op jit(solution)/shard_map/ppermute | solution.py:31
  246.7 10.6 collective-permute-done.10
  258.0 19.4 %collective-permute-done.11 = bf16[3,48,1536]{2,1,0:T(8,128)(2,1)S(1)} collective-permute-done((bf16[3,48,1536]{2,1,0:T(8,128)(2,1)S(1)}, bf16[3,48,1536]{2,1,0:T(8,128)(2,1)S(1)}, u32[]{:S(2)}, u32[]{:S(2)}) %collective-permute-start.11) | collective-permute-done | bytes 442400 | tf_op jit(solution)/shard_map/ppermute | solution.py:31
  277.4 18.9 %collective-permute-done.12 = bf16[3,48,1536]{2,1,0:T(8,128)(2,1)S(1)} collective-permute-done((bf16[3,48,1536]{2,1,0:T(8,128)(2,1)S(1)}, bf16[3,48,1536]{2,1,0:T(8,128)(2,1)S(1)}, u32[]{:S(2)}, u32[]{:S(2)}) %collective-permute-start.12) | collective-permute-done | bytes 442400 | tf_op jit(solution)/shard_map/ppermute | solution.py:31
  412.5 12.9 fusion.32
  425.4 20.1 %convert_reduce_fusion = (f32[10,1536]{1,0:T(8,128)}, bf16[10,128,1536]{2,1,0:T(8,128)(2,1)}) fusion(f32[10,128,1536]{2,1,0:T(8,128)} %get-tuple-element.101, f32[10,1536]{1,0:T(8,128)S(1)} %fusion.83, bf16[10,128,768]{2,1,0:T(8,128)(2,1)} %bitcast.103, bf16[10,768,768]{2,1,0:T(8,128)(2,1)} %gather_fusion.7, bf16[10,768,768]{2,1,0:T(8,128)(2,1)} %gather_fusion.6), kind=kOutput, calls=%fused_computation.38 | convolution fusion | flops 3092628480 | bytes 37478400 | tf_op jit(solution)/shard_map/pim,pmj->pij/dot_general | solution.py:203
  445.6 14.0 fusion.112
  468.7 20.0 %fusion.14 = bf16[10,128,1536]{2,1,0:T(8,128)(2,1)} fusion(f32[10,128,1536]{2,1,0:T(8,128)} %get-tuple-element.101, f32[10,1536]{1,0:T(8,128)S(1)} %fusion.83, u16[128,1536]{1,0:T(8,128)(2,1)S(1)} %get-tuple-element.67, u16[128,1536]{1,0:T(8,128)(2,1)S(1)} %get-tuple-element.66), kind=kLoop, calls=%fused_computation.26 | loop fusion | flops 139591680 | bytes 12644352 | tf_op jit(solution)/shard_map/convert_element_type | solution.py:170
  488.7 14.2 fusion.4
  514.2 20.6 %fusion.113 = f32[10,768,1536]{2,1,0:T(8,128)} fusion(bf16[10,128,768]{2,1,0:T(8,128)(2,1)} %bitcast.101, bf16[10,128,1536]{2,1,0:T(8,128)(2,1)} %get-tuple-element.105), kind=kOutput, calls=%fused_computation.219 | convolution fusion | flops 3019898880 | bytes 53084160 | tf_op jit(solution)/shard_map/jxa,jxm->jam/dot_general | solution.py:217
  583.9 66.8 %fusion.2 = f32[3,768,1536]{2,0,1:T(4,128)} fusion(f32[10,768,1536]{2,1,0:T(8,128)} %fusion.113, s32[10]{0:T(128)S(1)} %copy-done.41), kind=kOutput, calls=%fused_computation.12 | convolution fusion | flops 424673312 | bytes 61341736 | tf_op jit(solution)/shard_map/te,tdf->edf/dot_general | solution.py:220
  652.9 20.9 %fusion.114 = f32[10,768,1536]{2,1,0:T(8,128)} fusion(bf16[10,128,768]{2,1,0:T(8,128)(2,1)S(1)} %bitcast.104, bf16[10,128,1536]{2,1,0:T(8,128)(2,1)} %fusion.14), kind=kOutput, calls=%fused_computation.220 | convolution fusion | flops 3019898880 | bytes 53084160 | tf_op jit(solution)/shard_map/jxa,jxm->jam/dot_general | solution.py:213
  676.1 66.9 %fusion = f32[3,768,1536]{2,0,1:T(4,128)} fusion(f32[10,768,1536]{2,1,0:T(8,128)} %fusion.114, s32[10]{0:T(128)S(1)} %copy-done.41), kind=kOutput, calls=%fused_computation.10 | convolution fusion | flops 424673312 | bytes 61341736 | tf_op jit(solution)/shard_map/te,tdf->edf/dot_general | solution.py:216
  779.9 64.8 %all-reduce.4 = (f32[2,384]{1,0:T(2,128)}, f32[768]{0:T(1024)}, f32[3,1536]{1,0:T(4,128)}, f32[3,768]{1,0:T(4,128)}, f32[4,768]{1,0:T(4,128)}) all-reduce(f32[2,384]{1,0:T(2,128)S(1)} %pad_maximum_fusion.5, f32[768]{0:T(1024)S(1)} %get-tuple-element.84, f32[3,1536]{1,0:T(4,128)S(1)} %fusion.81, ...), channel_id=1, replica_groups=mesh['dp'=16,'rep'=2] {'dp'}, use_global_device_ids=true, to_apply=%region_29.30 | all-reduce | flops 11520 | bytes 92160 | tf_op jit(solution)/shard_map/psum | solution.py:295
  844.7 614.0 %all-reduce.8.cloned.1.call-done = (f32[3,768,384]{2,0,1:T(4,128)}, f32[3,768,1536]{2,0,1:T(4,128)}, f32[3,768,1536]{2,0,1:T(4,128)}) async-done(((f32[3,768,384]{2,0,1:T(4,128)}, f32[3,768,1536]{2,0,1:T(4,128)}, f32[3,768,1536]{2,0,1:T(4,128)}), (f32[3,768,384]{2,0,1:T(4,128)}, f32[3,768,1536]{2,0,1:T(4,128)}, f32[3,768,1536]{2,0,1:T(4,128)})) %all-reduce.8.cloned.1.call-update) | async-done | bytes 31850512
  1465.7 55.4 %reduce-scatter.14.cloned.1.call-done = f32[48,384]{1,0:T(8,128)} async-done(((f32[768,384]{1,0:T(8,128)}), f32[48,384]{1,0:T(8,128)}) %reduce-scatter.14.cloned.1.call-update) | async-done | bytes 73744 | tf_op jit(solution)/shard_map/reduce_scatter | solution.py:292
  (298 shorter events, 316.5 us)
Async XLA Ops:
  7.2 47.4 %all-gather.8.cloned.1.call-start = ((), (), s32[]{:S(2)}) async-start(), calls=%async_computation.5 | async-start | bytes 1880064 | tf_op jit(solution)/shard_map/all_gather | solution.py:109
  7.9 95.3 %reduce-scatter.16.cloned.1.call-start = ((), (), s32[]{:S(2)}) async-start(), calls=%async_computation.13 | async-start | bytes 2064384
  80.3 256.2 %all-gather.10.cloned.1.call-start = ((), (), s32[]{:S(2)}) async-start(), calls=%async_computation.6 | async-start | bytes 1806336 | tf_op jit(solution)/shard_map/all_gather | solution.py:141
  105.4 242.1 %all-gather.12.cloned.1.call-start = ((), (), s32[]{:S(2)}) async-start(), calls=%async_computation.7 | async-start | bytes 7520256 | tf_op jit(solution)/shard_map/all_gather | solution.py:156
  106.0 273.9 %all-gather.16.cloned.1.call-start = ((), (), s32[]{:S(2)}) async-start(), calls=%async_computation.9 | async-start | bytes 7520256 | tf_op jit(solution)/shard_map/all_gather | solution.py:191
  106.6 405.4 %reduce-scatter.20.cloned.1.call-start = ((), (), s32[]{:S(2)}) async-start(), calls=%async_computation.15 | async-start | bytes 2064384
  106.6 10.5 collective-permute-start
  127.5 10.4 collective-permute-start.2
  138.0 18.1 %collective-permute-start.3 = (bf16[3,48,1536]{2,1,0:T(8,128)(2,1)S(1)}, bf16[3,48,1536]{2,1,0:T(8,128)(2,1)S(1)}, u32[]{:S(2)}, u32[]{:S(2)}) collective-permute-start(bf16[3,48,1536]{2,1,0:T(8,128)(2,1)S(1)} %collective-permute-done.2), channel_id=1, source_target_pairs={{0,2},{2,4},{4,6},{6,8},{8,10},{10,12},{12,14},{14,16},{16,18},{18... | collective-permute-start | bytes 1327112 | tf_op jit(solution)/shard_map/ppermute | solution.py:31
  156.1 11.4 collective-permute-start.4
  167.5 18.8 %collective-permute-start.5 = (bf16[3,48,1536]{2,1,0:T(8,128)(2,1)}, bf16[3,48,1536]{2,1,0:T(8,128)(2,1)S(1)}, u32[]{:S(2)}, u32[]{:S(2)}) collective-permute-start(bf16[3,48,1536]{2,1,0:T(8,128)(2,1)} %collective-permute-done.4), channel_id=1, source_target_pairs={{0,2},{2,4},{4,6},{6,8},{8,10},{10,12},{12,14},{14,16},{16,18},{18... | collective-permute-start | bytes 1327112 | tf_op jit(solution)/shard_map/ppermute | solution.py:31
  186.2 16.3 %collective-permute-start.6 = (bf16[3,48,1536]{2,1,0:T(8,128)(2,1)S(1)}, bf16[3,48,1536]{2,1,0:T(8,128)(2,1)S(1)}, u32[]{:S(2)}, u32[]{:S(2)}) collective-permute-start(bf16[3,48,1536]{2,1,0:T(8,128)(2,1)S(1)} %collective-permute-done.5), channel_id=1, source_target_pairs={{0,2},{2,4},{4,6},{6,8},{8,10},{10,12},{12,14},{14,16},{16,18},{18... | collective-permute-start | bytes 1327112 | tf_op jit(solution)/shard_map/ppermute | solution.py:31
  202.5 13.6 collective-permute-start.7
  226.6 20.0 %collective-permute-start.9 = (bf16[3,48,1536]{2,1,0:T(8,128)(2,1)S(1)}, bf16[3,48,1536]{2,1,0:T(8,128)(2,1)S(1)}, u32[]{:S(2)}, u32[]{:S(2)}) collective-permute-start(bf16[3,48,1536]{2,1,0:T(8,128)(2,1)S(1)} %collective-permute-done.8), channel_id=1, source_target_pairs={{0,2},{2,4},{4,6},{6,8},{8,10},{10,12},{12,14},{14,16},{16,18},{18... | collective-permute-start | bytes 1327112 | tf_op jit(solution)/shard_map/ppermute | solution.py:31
  246.6 10.7 collective-permute-start.10
  257.3 20.0 %collective-permute-start.11 = (bf16[3,48,1536]{2,1,0:T(8,128)(2,1)S(1)}, bf16[3,48,1536]{2,1,0:T(8,128)(2,1)S(1)}, u32[]{:S(2)}, u32[]{:S(2)}) collective-permute-start(bf16[3,48,1536]{2,1,0:T(8,128)(2,1)S(1)} %collective-permute-done.10), channel_id=1, source_target_pairs={{0,2},{2,4},{4,6},{6,8},{8,10},{10,12},{12,14},{14,16},{16,18},{18... | collective-permute-start | bytes 1327112 | tf_op jit(solution)/shard_map/ppermute | solution.py:31
  277.3 19.0 %collective-permute-start.12 = (bf16[3,48,1536]{2,1,0:T(8,128)(2,1)S(1)}, bf16[3,48,1536]{2,1,0:T(8,128)(2,1)S(1)}, u32[]{:S(2)}, u32[]{:S(2)}) collective-permute-start(bf16[3,48,1536]{2,1,0:T(8,128)(2,1)S(1)} %collective-permute-done.11), channel_id=1, source_target_pairs={{0,2},{2,4},{4,6},{6,8},{8,10},{10,12},{12,14},{14,16},{16,18},{18... | collective-permute-start | bytes 1327112 | tf_op jit(solution)/shard_map/ppermute | solution.py:31
  468.6 66.4 %all-gather.18.cloned.1.call-start = ((), (), s32[]{:S(2)}) async-start(), calls=%async_computation.10 | async-start | bytes 1806336 | tf_op jit(solution)/shard_map/all_gather | solution.py:230
  514.2 136.5 %reduce-scatter.18.cloned.1.call-start = ((), (), s32[]{:S(2)}) async-start(), calls=%async_computation.14 | async-start | bytes 2064384
  534.8 138.9 %reduce-scatter.22.cloned.1.call-start = ((), (), s32[]{:S(2)}) async-start(), calls=%async_computation.16 | async-start | bytes 2064384
  583.8 174.6 %all-gather.14.cloned.1.call-start = ((), (), s32[]{:S(2)}) async-start(), calls=%async_computation.8 | async-start | bytes 1806336 | tf_op jit(solution)/shard_map/all_gather | solution.py:178
  652.8 117.5 %all-gather.20.cloned.1.call-start = ((), (), s32[]{:S(2)}) async-start(), calls=%async_computation.11 | async-start | bytes 1806336 | tf_op jit(solution)/shard_map/all_gather | solution.py:284
  676.1 782.6 %all-reduce.8.cloned.1.call-start = ((), (), s32[]{:S(2)}) async-start(), calls=%async_computation.17 | async-start | bytes 84934656
  754.8 766.2 %reduce-scatter.14.cloned.1.call-start = ((), (), s32[]{:S(2)}) async-start(), calls=%async_computation.12 | async-start | bytes 1253376 | tf_op jit(solution)/shard_map/reduce_scatter | solution.py:292
  (53 other events, 2357.0 us)
Sparse Core Ops, SparseCore 0:
  10.3 44.2 all-gather.7
  80.5 22.7 reduce-scatter.15
  105.5 23.0 all-gather.9
  130.7 79.6 all-gather.11
  212.6 81.4 all-gather.15
  468.8 21.2 reduce-scatter.19
  514.3 20.1 all-gather.17
  536.8 23.9 reduce-scatter.17
  583.9 23.4 reduce-scatter.21
  653.0 22.4 all-gather.13
  677.0 23.0 all-gather.19
  754.9 703.6 all-reduce.7
  1462.9 58.1 reduce-scatter.13
